TPU v7x, 32 devices: a whole 2x2x4 slice. The times are simulated.
32 devices in a mesh: dp: 2 (over x), ep: 4 (over z), tp: 4 (over y, core).
Axes of the slice: x: 2, y: 2, z: 4, core: 2. Of those that a mesh axis runs over, the one named last changes fastest.
Arguments:
- x: bfloat16 [2048, 2048], P(('dp', 'ep')), parts along dimension 0
- idx: int32 [2048, 6], P(('dp', 'ep')), parts along dimension 0
- g: float32 [2048, 6], P(('dp', 'ep')), parts along dimension 0
- w1: bfloat16 [64, 2048, 1408], P('ep', None, 'tp')
- w3: bfloat16 [64, 2048, 1408], P('ep', None, 'tp')
- w2: bfloat16 [64, 1408, 2048], P('ep', 'tp')
Outputs:
- output: bfloat16 [2048, 2048], P(('dp', 'ep')), parts along dimension 0
There are 2 independent parts. A program takes and returns all parts, laid end to end along the dimension named above; an argument that names none is the same for every part.
All inputs are finite; a program needn't handle non-finite values.
Results may differ from a plain program's by a relative error of at most 0.0100673.
Values are sent between devices in bfloat16 or wider.
A program may use at most 1 GiB of HBM per device.

v0:
```python
import jax
import jax.numpy as jnp
from jax import lax
from jax.sharding import PartitionSpec as P

CF = 2


def _dest(idx, E, C):
    e = idx.reshape(-1)
    oh = jax.nn.one_hot(e, E, dtype=jnp.int32)
    slot = jnp.sum((jnp.cumsum(oh, axis=0) - oh) * oh, axis=1)
    return jnp.where(slot < C, e * C + slot, E * C)


def solution(mesh):
    nep, ntp = mesh.shape["ep"], mesh.shape["tp"]
    tok = P(("dp", "ep"), None)

    def body(x, idx, g, w1, w3, w2):
        TL, D = x.shape
        K = idx.shape[1]
        EL = w1.shape[0]
        E = EL * nep
        C = CF * K * TL // E
        Cq = C // ntp
        dest = _dest(idx, E, C)
        buf = jnp.zeros((E * C, D), x.dtype).at[dest].set(jnp.repeat(x, K, axis=0), mode="drop")
        recv = lax.all_to_all(buf.reshape(nep, EL, C, D), "ep", 0, 0, tiled=True)
        xe = recv.transpose(1, 0, 2, 3).reshape(EL, nep * C, D)
        h1 = jnp.einsum("esd,edf->esf", xe, w1, preferred_element_type=jnp.float32)
        h3 = jnp.einsum("esd,edf->esf", xe, w3, preferred_element_type=jnp.float32)
        h = (jax.nn.silu(h1) * h3).astype(jnp.bfloat16)
        yp = jnp.einsum("esf,efd->esd", h, w2, preferred_element_type=jnp.float32).astype(jnp.bfloat16)
        yp = lax.all_to_all(yp.reshape(EL, nep, ntp, Cq, D), "tp", 2, 2, tiled=True)
        y = jnp.sum(yp, axis=2, dtype=jnp.float32).astype(jnp.bfloat16)
        back = lax.all_to_all(y, "ep", 1, 1, tiled=True)
        back = back.transpose(1, 0, 2, 3).reshape(E, Cq, D)
        yall = lax.all_gather(back, "tp", axis=1, tiled=True).reshape(E * C, D)
        yc = jnp.take(yall, dest, axis=0, mode="fill", fill_value=0).reshape(TL, K, D)
        out = jnp.sum(yc.astype(jnp.float32) * g[:, :, None], axis=1)
        return out.astype(jnp.bfloat16)

    return jax.shard_map(
        body,
        mesh=mesh,
        in_specs=(tok, tok, tok, P("ep", None, "tp"), P("ep", None, "tp"), P("ep", "tp", None)),
        out_specs=tok,
        check_vma=False,
    )
```

profile of v0, /device:TPU:0, one launch (start us, length us, event | category | flops | bytes accessed | tf_op | source)
XLA Modules:
  0.0 773.0 jit_solution(168768831938769119)
XLA Ops:
  6.5 0.8 copy.28
  7.4 0.1 eq.36
  7.5 0.1 eq.32
  7.7 18.1 %reduce-window.6 = s32[64,12,128]{2,1,0:T(8,128)S(1)} reduce-window(s32[64,12,128]{2,1,0:T(8,128)S(1)} %fusion.3, s32[]{:T(128)} %constant.13.clone.1), window={size=1x1x128 pad=0_0x0_0x127_0}, to_apply=%region_0.1 | reduce-window | flops 12484608 | bytes 786436 | tf_op jit(solution)/shard_map/reduce-window
  25.9 0.2 slice.10
  26.1 0.3 copy.30
  26.4 0.1 copy.31
  26.5 0.2 broadcast_add_fusion
  26.7 0.1 mul.36
  26.8 6.0 broadcast_in_dim.30
  32.8 11.1 %reshape.105 = bf16[1536,2048]{1,0:T(8,128)(2,1)} reshape(bf16[256,6,2048]{2,1,0:T(8,128)(2,1)} %broadcast_in_dim.30) | data formatting | bytes 12582912 | tf_op jit(solution)/shard_map/reshape | solution.py:28
  43.9 0.2 fusion.6
  44.1 17.4 %scatter_custom_fusion = bf16[3072,2048]{1,0:T(8,128)(2,1)} fusion(s32[1536]{0:T(1024)S(1)} %fusion.7, bf16[1536,2048]{1,0:T(8,128)(2,1)} %reshape.105, bf16[]{:T(256)} %constant.30.clone.1), kind=kCustom, calls=%fused_computation.4 | custom fusion | bytes 12583424 | tf_op jit(solution)/shard_map/scatter | solution.py:28
  61.5 279.0 %all_to_all.15 = bf16[4,16,48,2048]{3,2,1,0:T(8,128)(2,1)S(1)} all-to-all(bf16[4,16,48,2048]{3,2,1,0:T(8,128)(2,1)} %bitcast.33), channel_id=1, replica_groups=mesh['dp'=2,'ep'=4,'tp'=4] {'ep'}, dimensions={0} | all-to-all | bytes 25165824 | tf_op jit(solution)/shard_map/all_to_all | solution.py:29
  340.5 5.2 copy.33
  345.7 17.2 %fusion.11 = f32[16,192,352]{2,1,0:T(8,128)} fusion(bf16[16,192,2048]{2,1,0:T(8,128)(2,1)} %bitcast.36, bf16[16,2048,352]{1,2,0:T(8,128)(2,1)} %param.9), kind=kOutput, calls=%fused_computation.25 | convolution fusion | flops 4429185024 | bytes 39976960 | tf_op jit(solution)/shard_map/esd,edf->esf/dot_general | solution.py:31
  362.9 27.3 %convolution_convert_fusion = bf16[16,192,2048]{2,1,0:T(8,128)(2,1)} fusion(bf16[16,352,2048]{2,1,0:T(8,128)(2,1)} %param.11, f32[16,192,352]{2,1,0:T(8,128)} %fusion.11, bf16[16,192,2048]{2,1,0:T(8,128)(2,1)} %bitcast.37, bf16[16,2048,352]{1,2,0:T(8,128)(2,1)} %param.10), kind=kOutput, calls=%fused_computation.3 | convolution fusion | flops 8871149568 | bytes 75628544 | tf_op jit(solution)/shard_map/esf,efd->esd/dot_general | solution.py:34
  390.1 11.7 %copy.34 = bf16[16,192,2048]{2,0,1:T(8,128)(2,1)S(1)} copy(bf16[16,192,2048]{2,1,0:T(8,128)(2,1)} %convolution_convert_fusion) | data formatting | bytes 25165824 | tf_op jit(solution)/shard_map/convert_element_type | solution.py:34
  401.9 1.9 copy.35
  403.8 142.0 %all_to_all.16 = bf16[16,4,4,12,2048]{4,0,3,1,2:T(8,128)(2,1)} all-to-all(bf16[16,4,4,12,2048]{4,0,3,1,2:T(8,128)(2,1)S(1)} %copy.35), channel_id=1, replica_groups=mesh['dp'=2,'ep'=4,'tp'=4] {'tp'}, dimensions={2} | all-to-all | bytes 25165824 | tf_op jit(solution)/shard_map/all_to_all | solution.py:35
  545.9 8.4 %reduce_sum.37 = bf16[16,4,12,2048]{3,0,2,1:T(8,128)(2,1)S(1)} reduce(bf16[16,4,4,12,2048]{4,0,3,1,2:T(8,128)(2,1)} %all_to_all.16, bf16[]{:T(256)} %constant.30.clone.1), dimensions={2}, to_apply=%region_4.5 | reduce | flops 4718592 | bytes 15728642 | tf_op jit(solution)/shard_map/reduce_sum | solution.py:36
  554.3 73.1 %all_to_all.17 = bf16[16,4,12,2048]{3,0,2,1:T(8,128)(2,1)S(1)} all-to-all(bf16[16,4,12,2048]{3,0,2,1:T(8,128)(2,1)S(1)} %reduce_sum.37), channel_id=1, replica_groups=mesh['dp'=2,'ep'=4,'tp'=4] {'ep'}, dimensions={1} | all-to-all | bytes 6291456 | tf_op jit(solution)/shard_map/all_to_all | solution.py:37
  627.3 2.1 copy.37
  629.4 0.0 all-gather.2.cloned.1.call-update
  629.4 0.1 reduce_sum.35
  629.6 0.1 copy.39
  629.8 0.1 compare_and_fusion
  629.8 80.6 %all-gather.2.cloned.1.call-done = bf16[64,48,2048]{2,0,1:T(8,128)(2,1)} async-done(((bf16[64,12,2048]{2,0,1:T(8,128)(2,1)}), bf16[64,48,2048]{2,0,1:T(8,128)(2,1)}) %all-gather.2.cloned.1.call-update) | async-done | bytes 12582928 | tf_op jit(solution)/shard_map/all_gather | solution.py:39
  710.4 14.5 %copy.38 = bf16[64,48,2048]{2,1,0:T(8,128)(2,1)} copy(bf16[64,48,2048]{2,0,1:T(8,128)(2,1)} %all-gather.2.cloned.1.call-done) | data formatting | bytes 25165824 | tf_op jit(solution)/shard_map/all_gather | solution.py:39
  724.9 18.9 %gather_fusion = bf16[1536,2048]{1,0:T(8,128)(2,1)} fusion(bf16[3072,2048]{1,0:T(8,128)(2,1)} %bitcast.32, s32[2048]{0:T(1024)S(1)} %pad_clamp_fusion), kind=kCustom, calls=%fused_computation | custom fusion | bytes 12589056 | tf_op jit(solution)/shard_map/jit(_take)/gather | solution.py:40
  743.9 10.9 %gather.7 = bf16[256,6,2048]{2,1,0:T(8,128)(2,1)} reshape(bf16[1536,2048]{1,0:T(8,128)(2,1)} %gather_fusion) | data formatting | bytes 12582912 | tf_op jit(solution)/shard_map/jit(_take)/gather | solution.py:40
  754.8 11.4 %multiply_reduce_fusion = bf16[256,2048]{1,0:T(8,128)(2,1)} fusion(f32[256,6]{1,0:T(8,128)S(1)} %copy.39, bf16[256,6,2048]{2,1,0:T(8,128)(2,1)} %gather.7, pred[256,6]{1,0:T(8,128)(4,1)S(1)} %compare_and_fusion), kind=kLoop, calls=%fused_computation.2 | loop fusion | flops 12058624 | bytes 7347712 | tf_op jit(solution)/shard_map/reduce_sum | solution.py:41
  (8 shorter events, 0.1 us)
Async XLA Ops:
  6.5 703.9 %all-gather.2.cloned.1.call-start = ((), (), s32[]{:S(2)}) async-start(), calls=%async_computation.3 | async-start | bytes 15728640 | tf_op jit(solution)/shard_map/all_gather | solution.py:39
  545.9 83.7 %copy-start = (f32[256,6]{0,1:T(8,128)S(1)}, f32[256,6]{0,1:T(8,128)}, u32[]{:S(2)}) copy-start(f32[256,6]{0,1:T(8,128)} %param.8) | copy-start | bytes 18436
Sparse Core Ops, SparseCore 0:
  629.6 80.8 all-gather.1
where the time goes:
time: 774 us; the launch traced here: 773 us
  blocking collectives  494 us (64%)
  local copies, waits for them, and re-layouts  102 us (13%)
  waiting for transfers between devices  80.6 us (10%)
  matrix products  44.5 us (6%)
  other arithmetic  38.5 us (5%)
  between operations  13.5 us (2%)
    all_to_all x1, blocking collectives, body(): recv = lax.all_to_all(buf.reshape(nep, EL, C, D), 'ep', 0, 0, tiled=True)  279 us
    all_to_all x1, blocking collectives, body(): yp = lax.all_to_all(yp.reshape(EL, nep, ntp, Cq, D), 'tp', 2, 2, tiled=True)  142 us
    all_gather x1, waiting for transfers between devices, body(): yall = lax.all_gather(back, 'tp', axis=1, tiled=True).reshape(E * C, D)  80.6 us
    all_to_all x1, blocking collectives, body(): back = lax.all_to_all(y, 'ep', 1, 1, tiled=True)  73.1 us
    gather x2, local copies, waits for them, and re-layouts, body(): jnp.take(yall, dest, axis=0, mode='fill', fill_value=0).reshape(TL, K, D)  29.9 us
    dot_general x1, matrix products, body(): jnp.einsum('esf,efd->esd', h, w2, preferred_element_type=jnp.float32)  27.3 us
    another operation x3, other arithmetic  18.4 us
    scatter x1, local copies, waits for them, and re-layouts, body(): jnp.zeros((E * C, D), x.dtype).at[dest]  17.4 us
  transfers between devices with their start and end apart: 1, of which 1 were waited for; matrix products, arithmetic and copies ran while one was open for 0% of the time, Pallas kernels for 0%

commit v1 on v0

v1 whole, which is shorter than its diff:
```python
import functools

import jax
import jax.numpy as jnp
from jax import lax
from jax.experimental import pallas as pl
from jax.experimental.pallas import tpu as pltpu
from jax.sharding import PartitionSpec as P

MESH = pl.DeviceIdType.MESH
CF = 2
BF = jnp.bfloat16
F32 = jnp.float32
VMEM_LIMIT = 64 * 1000 * 1000


def _peers():
    z, t = lax.axis_index("ep"), lax.axis_index("tp")
    zs = (3 - z, lax.rem(z + 2, 4), z + 1 - 2 * lax.rem(z, 2))
    yq = lax.rem(t + 2, 4)
    cq = t + 1 - 2 * lax.rem(t, 2)
    return z, t, zs, yq, cq


def _entry_barrier(zs, yq, cq):
    bar = pltpu.get_barrier_semaphore()
    for p in zs:
        pl.semaphore_signal(bar, inc=1, device_id={"ep": p}, device_id_type=MESH)
    for p in (yq, cq):
        pl.semaphore_signal(bar, inc=1, device_id={"tp": p}, device_id_type=MESH)
    pl.semaphore_wait(bar, 5)


def _rcopy(src, dst, ss, rs, dev):
    return pltpu.make_async_remote_copy(
        src_ref=src, dst_ref=dst, send_sem=ss, recv_sem=rs, device_id=dev, device_id_type=MESH
    )


def _gather_kernel(x_ref, rt_ref, xall_ref, rtall_ref, xb, rb, sem, lsem, rsem):
    z, t, zs, yq, cq = _peers()
    nr = x_ref.shape[0] // 4
    own = pltpu.make_async_copy(x_ref, xb.at[z], lsem.at[0])
    own.start()
    ownr = pltpu.make_async_copy(rt_ref, rb.at[z], lsem.at[1])
    ownr.start()
    _entry_barrier(zs, yq, cq)
    own.wait()
    ownr.wait()

    def rows(s, q):
        return xb.at[s, pl.ds(pl.multiple_of(q * nr, nr), nr)]

    zc, rc = [], []
    for i, p in enumerate(zs):
        c = _rcopy(rows(z, t), rows(z, t), sem.at[0, i], sem.at[1, i], {"ep": p})
        c.start()
        zc.append(c)
        r = _rcopy(rb.at[z], rb.at[z], rsem.at[0, i], rsem.at[1, i], {"ep": p})
        r.start()
        rc.append(r)
    yc, dc, ec = [], [], []
    for i, p in enumerate(zs):
        zc[i].wait_recv()
        c = _rcopy(rows(p, t), rows(p, t), sem.at[2, i], sem.at[3, i], {"tp": yq})
        c.start()
        yc.append(c)
        c = _rcopy(rows(p, t), rows(p, t), sem.at[4, i], sem.at[5, i], {"tp": cq})
        c.start()
        dc.append(c)
    for i, p in enumerate(zs):
        yc[i].wait_recv()
        c = _rcopy(rows(p, yq), rows(p, yq), sem.at[6, i], sem.at[7, i], {"tp": cq})
        c.start()
        ec.append(c)
    for c in rc:
        c.wait()
    for i in range(3):
        dc[i].wait_recv()
        ec[i].wait_recv()
    o = pltpu.make_async_copy(xb, xall_ref, lsem.at[0])
    o.start()
    rtall_ref[...] = rb[...]
    for c in zc + yc + dc + ec:
        c.wait_send()
    o.wait()


def _members(rt, el, ebase, k):
    tl = rt.shape[1]
    eid = lax.broadcasted_iota(jnp.int32, (el, tl), 0) + ebase
    m = jnp.zeros((el, tl), F32)
    gm = jnp.zeros((el, tl), F32)
    for j in range(k):
        hit = rt[j : j + 1, :].astype(jnp.int32) == eid
        m = jnp.where(hit, 1.0, m)
        gm = jnp.where(hit, rt[8 + j : 9 + j, :], gm)
    a = lax.broadcasted_iota(jnp.int32, (tl, tl), 0)
    b = lax.broadcasted_iota(jnp.int32, (tl, tl), 1)
    u = jnp.where(a < b, 1.0, 0.0).astype(BF)
    slot = jnp.dot(m.astype(BF), u, preferred_element_type=F32)
    return jnp.where(m > 0, slot, -1.0), gm


def _expert_kernel(k, cap, rt_ref, x_ref, w1_ref, w3_ref, h_ref, xe, pm):
    e = pl.program_id(0)
    el = xe.shape[0]
    ns, tl, d = x_ref.shape
    ebase = lax.axis_index("ep") * el

    @pl.when(e == 0)
    def _():
        ci = lax.broadcasted_iota(jnp.int32, (cap, tl), 0).astype(F32)

        @pl.loop(0, ns)
        def _(s):
            slot, _g = _members(rt_ref[s], el, ebase, k)
            for i in range(el):
                pm[i * cap : (i + 1) * cap, :] = jnp.where(slot[i : i + 1, :] == ci, 1.0, 0.0).astype(BF)

            @pl.loop(0, d // 256)
            def _(n):
                cs = pl.ds(pl.multiple_of(n * 256, 256), 256)
                v = jnp.dot(pm[...], x_ref[s, :, cs], preferred_element_type=F32).astype(BF)
                xe[:, pl.ds(pl.multiple_of(s * cap, cap), cap), cs] = v.reshape(el, cap, 256)

    xv = xe[e]
    a = jnp.dot(xv, w1_ref[0], preferred_element_type=F32)
    b = jnp.dot(xv, w3_ref[0], preferred_element_type=F32)
    h_ref[0] = (jax.nn.silu(a) * b).astype(BF)


NB = 256


def _combine_kernel(k, cap, rt_ref, h_ref, w2_ref, y_ref, gt, w2b, ypb, part, drecv, ysend, yrecv, zrecv, yb, wsem, dsem, ysem, zsem, fsem):
    z, t, zs, yq, cq = _peers()
    el, ns = h_ref.shape[0], rt_ref.shape[0]
    tl = rt_ref.shape[2]
    ebase = z * el
    sord = zs + (z,)
    own4 = (lax.rem(cq + 2, 4), yq, cq, t)
    cols = [own4[kd] * 512 + n * NB for n in range(2) for kd in range(4)]

    def wcopy(b):
        return pltpu.make_async_copy(
            w2_ref.at[:, :, pl.ds(pl.multiple_of(cols[b], NB), NB)], w2b.at[b % 2], wsem.at[b % 2]
        )

    wcopy(0).start()
    _entry_barrier(zs, yq, cq)

    ci = lax.broadcasted_iota(jnp.int32, (cap, tl), 0).astype(F32)

    @pl.loop(0, ns)
    def _(s):
        slot, gm = _members(rt_ref[s], el, ebase, k)
        gf = jnp.concatenate(
            [jnp.where(slot[i : i + 1, :] == ci, gm[i : i + 1, :], 0.0) for i in range(el)], axis=0
        )
        g = gf.T
        hi = g.astype(BF)
        r = g - hi.astype(F32)
        mid = r.astype(BF)
        gt[s, 0] = hi
        gt[s, 1] = mid
        gt[s, 2] = (r - mid.astype(F32)).astype(BF)

    def compute(b):
        wcopy(b).wait()
        if b + 1 < 8:
            wcopy(b + 1).start()
        sl = b % 2

        @pl.loop(0, el, step=4)
        def _(e0):
            for i in range(4):
                e = e0 + i
                v = jnp.dot(h_ref[e], w2b[sl, e], preferred_element_type=F32).astype(BF)
                ypb[:, pl.ds(pl.multiple_of(e * cap, cap), cap), :] = v.reshape(ns, cap, NB)

        @pl.loop(0, ns)
        def _(s):
            yp = ypb[s]
            acc = jnp.dot(gt[s, 0], yp, preferred_element_type=F32)
            acc += jnp.dot(gt[s, 1], yp, preferred_element_type=F32)
            acc += jnp.dot(gt[s, 2], yp, preferred_element_type=F32)
            part[b, s] = acc

    def dcopy(n, j):
        return _rcopy(part.at[n * 4 + 2 * j], drecv.at[n, j], dsem.at[0, n, j], dsem.at[1, n, j], {"tp": cq})

    def ycopy(n, i):
        return _rcopy(ysend.at[n, sord[i]], yrecv.at[n, sord[i]], ysem.at[0, n, i], ysem.at[1, n, i], {"tp": yq})

    def zcopy(n, i):
        return _rcopy(ysend.at[n, 4 + i], zrecv.at[n, i], zsem.at[0, n, i], zsem.at[1, n, i], {"ep": zs[i]})

    def ystep(n):
        dcopy(n, 0).wait_recv()
        for i in range(4):
            s = sord[i]
            ysend[n, s] = part[n * 4 + 1, s] + drecv[n, 0, s]
        for i in range(4):
            ycopy(n, i).start()

    def zstep(n, i):
        s = sord[i]
        ycopy(n, i).wait_recv()
        ysend[n, 4 + i] = part[n * 4 + 3, s] + drecv[n, 1, s] + yrecv[n, s]
        if i < 3:
            zcopy(n, i).start()

    def fcopy(j, n, q, dev):
        sl = pl.ds(pl.multiple_of(q * 512 + n * NB, NB), NB)
        return _rcopy(yb.at[:, sl], yb.at[:, sl], fsem.at[0, n, j], fsem.at[1, n, j], {"tp": dev})

    def finish(n):
        acc = ysend[n, 7]
        for i in range(3):
            zcopy(n, i).wait_recv()
            acc += zrecv[n, i]
        yb[:, pl.ds(pl.multiple_of(t * 512 + n * NB, NB), NB)] = acc.astype(BF)

    def spread(n):
        fcopy(0, n, t, yq).start()
        fcopy(1, n, t, cq).start()

    compute(0)
    dcopy(0, 0).start()
    compute(1)
    ystep(0)
    compute(2)
    dcopy(0, 1).start()
    compute(3)
    dcopy(0, 1).wait_recv()
    zstep(0, 0)
    compute(4)
    dcopy(1, 0).start()
    compute(5)
    ystep(1)
    zstep(0, 1)
    compute(6)
    dcopy(1, 1).start()
    zstep(0, 2)
    compute(7)
    dcopy(1, 1).wait_recv()
    zstep(0, 3)
    zstep(1, 0)
    zstep(1, 1)
    finish(0)
    zstep(1, 2)
    spread(0)
    zstep(1, 3)
    finish(1)
    spread(1)
    for n in range(2):
        fcopy(0, n, t, yq).wait_recv()
        fcopy(2, n, yq, cq).start()
    for n in range(2):
        for j in range(2):
            dcopy(n, j).wait_send()
        for i in range(4):
            ycopy(n, i).wait_send()
        for i in range(3):
            zcopy(n, i).wait_send()
    for n in range(2):
        fcopy(1, n, t, cq).wait_recv()
        fcopy(2, n, yq, cq).wait_recv()
        for j in range(3):
            fcopy(j, n, t, cq).wait_send()
    y_ref[...] = yb[...]


def solution(mesh):
    tok = P(("dp", "ep"), None)
    nep = mesh.shape["ep"]

    def body(x, idx, g, w1, w3, w2):
        tl, d = x.shape
        k = idx.shape[1]
        el, _, fl = w1.shape
        cap = CF * k * tl // (el * nep)
        pad = jnp.zeros((8 - k, tl), F32)
        rt = jnp.concatenate([idx.T.astype(F32), pad, g.T, pad], axis=0)
        vm = pl.BlockSpec(memory_space=pltpu.VMEM)
        hbm = pl.BlockSpec(memory_space=pl.ANY)
        dma = pltpu.SemaphoreType.DMA
        xall, rtall = pl.pallas_call(
            _gather_kernel,
            out_shape=(jax.ShapeDtypeStruct((nep, tl, d), BF), jax.ShapeDtypeStruct((nep, 16, tl), F32)),
            in_specs=[hbm, hbm],
            out_specs=(hbm, vm),
            scratch_shapes=[
                pltpu.VMEM((nep, tl, d), BF),
                pltpu.VMEM((nep, 16, tl), F32),
                dma((8, 3)),
                dma((2,)),
                dma((2, 3)),
            ],
            compiler_params=pltpu.CompilerParams(collective_id=0, has_side_effects=True),
        )(x, rt)
        h = pl.pallas_call(
            functools.partial(_expert_kernel, k, cap),
            grid=(el,),
            out_shape=jax.ShapeDtypeStruct((el, nep * cap, fl), BF),
            in_specs=[
                pl.BlockSpec((nep, 16, tl), lambda e: (0, 0, 0)),
                pl.BlockSpec((nep, tl, d), lambda e: (0, 0, 0)),
                pl.BlockSpec((1, d, fl), lambda e: (e, 0, 0)),
                pl.BlockSpec((1, d, fl), lambda e: (e, 0, 0)),
            ],
            out_specs=pl.BlockSpec((1, nep * cap, fl), lambda e: (e, 0, 0)),
            scratch_shapes=[pltpu.VMEM((el, nep * cap, d), BF), pltpu.VMEM((el * cap, tl), BF)],
            compiler_params=pltpu.CompilerParams(vmem_limit_bytes=VMEM_LIMIT),
        )(rtall, xall, w1, w3)
        y = pl.pallas_call(
            functools.partial(_combine_kernel, k, cap),
            out_shape=jax.ShapeDtypeStruct((tl, d), BF),
            in_specs=[vm, vm, hbm],
            out_specs=vm,
            scratch_shapes=[
                pltpu.VMEM((nep, 3, tl, el * cap), BF),
                pltpu.VMEM((2, el, fl, NB), BF),
                pltpu.VMEM((nep, el * cap, NB), BF),
                pltpu.VMEM((8, nep, tl, NB), F32),
                pltpu.VMEM((2, 2, nep, tl, NB), F32),
                pltpu.VMEM((2, 8, tl, NB), F32),
                pltpu.VMEM((2, nep, tl, NB), F32),
                pltpu.VMEM((2, 3, tl, NB), F32),
                pltpu.VMEM((tl, d), BF),
                dma((2,)),
                dma((2, 2, 2)),
                dma((2, 2, 4)),
                dma((2, 2, 3)),
                dma((2, 2, 3)),
            ],
            compiler_params=pltpu.CompilerParams(
                collective_id=1, has_side_effects=True, vmem_limit_bytes=VMEM_LIMIT
            ),
        )(rtall, h, w2)
        return y

    return jax.shard_map(
        body,
        mesh=mesh,
        in_specs=(tok, tok, tok, P("ep", None, "tp"), P("ep", None, "tp"), P("ep", "tp", None)),
        out_specs=tok,
        check_vma=False,
    )
```

time: 774 us -> 222 us (0.29)
  blocking collectives: 494 us -> 0 us
  Pallas kernels: 0 us -> 157 us
  waiting for transfers between devices: 80.6 us -> 0 us
  matrix products: 44.5 us -> 0 us
  local copies, waits for them, and re-layouts: 102 us -> 61 us
  other arithmetic: 38.5 us -> 2.01 us
  between operations: 13.5 us -> 0.02 us
    all_to_all x3 -> x0, blocking collectives: 494 us -> none  [the longest x1 279 us: body(): recv = lax.all_to_all(buf.reshape(nep, EL, C, D), 'ep', 0, 0, tiled=True)]
    pallas_call x0 -> x3, Pallas kernels: none -> 157 us  [the longest x1 74.7 us: body(): pl.pallas_call(functools.partial(_combine_kernel, k, cap), out_shape=jax....]
    all_gather x1 -> x0, waiting for transfers between devices: 80.6 us -> none  [body(): yall = lax.all_gather(back, 'tp', axis=1, tiled=True).reshape(E * C, D)]
    unnamed x4 -> x3, local copies, waits for them, and re-layouts: 0.96 us -> 61 us
    dot_general x2 -> x0, matrix products: 44.5 us -> none  [the longest x1 27.3 us: body(): jnp.einsum('esf,efd->esd', h, w2, preferred_element_type=jnp.float32)]
    gather x2 -> x0, local copies, waits for them, and re-layouts: 29.9 us -> none  [body(): jnp.take(yall, dest, axis=0, mode='fill', fill_value=0).reshape(TL, K, D)]
    reduce_sum x3 -> x0, other arithmetic: 19.9 us -> none  [the longest x1 11.4 us: body(): out = jnp.sum(yc.astype(jnp.float32) * g[:, :, None], axis=1)]
    another operation x3 -> x0, other arithmetic: 18.4 us -> none
  transfers between devices with their start and end apart: 1 -> 0, of which waited for: 1 -> 0; matrix products, arithmetic and copies ran while one was open for 0% -> 0% of each run, Pallas kernels for 0% -> 0%
where the time goes in v1:
time: 222 us; the launch traced here: 220 us
  Pallas kernels  157 us (71%)
  local copies, waits for them, and re-layouts  61 us (27%)
    pallas_call x1, Pallas kernels, body(): pl.pallas_call(functools.partial(_combine_kernel, k, cap), out_shape=jax....  74.7 us
    unnamed x3, local copies, waits for them, and re-layouts  61 us
    pallas_call x1, Pallas kernels, body(): pl.pallas_call(_gather_kernel, out_shape=(jax.ShapeDtypeStruct((nep, tl,...  45.1 us
    pallas_call x1, Pallas kernels, body(): pl.pallas_call(functools.partial(_expert_kernel, k, cap), grid=(el,), out...  37 us

profile of v1, /device:TPU:0, one launch (start us, length us, event | category | flops | bytes accessed | tf_op | source)
XLA Modules:
  0.0 219.8 jit_solution(2576268308457750513)
XLA Ops:
  0.0 0.7 convert_bitcast_fusion
  0.7 1.3 pad_maximum_fusion.rt_ref
  2.0 45.1 %shard_map.64 = (bf16[4,256,2048]{2,1,0:T(8,128)(2,1)}, f32[4,16,256]{2,1,0:T(8,128)}) custom-call(bf16[256,2048]{1,0:T(8,128)(2,1)} %x_ref.1, f32[16,256]{1,0:T(8,128)} %pad_maximum_fusion.rt_ref), custom_call_target="tpu_custom_call" | custom-call | tf_op jit(solution)/shard_map/pallas_call | solution.py:289
  47.1 29.6 %copy.7.w1_ref = bf16[16,2048,352]{2,1,0:T(8,128)(2,1)} copy(bf16[16,2048,352]{1,2,0:T(8,128)(2,1)} %param.9) | data formatting | bytes 46137344 | tf_op args[3]
  76.8 29.1 %copy.8.w3_ref = bf16[16,2048,352]{2,1,0:T(8,128)(2,1)} copy(bf16[16,2048,352]{1,2,0:T(8,128)(2,1)} %param.10) | data formatting | bytes 46137344 | tf_op args[4]
  105.9 37.0 %shard_map.65.h_ref = bf16[16,192,352]{2,1,0:T(8,128)(2,1)} custom-call(f32[4,16,256]{2,1,0:T(8,128)} %get-tuple-element.7.rt_ref, bf16[4,256,2048]{2,1,0:T(8,128)(2,1)} %get-tuple-element.8.x_ref, bf16[16,2048,352]{2,1,0:T(8,128)(2,1)} %copy.7.w1_ref, bf16[16,2048,352]{2,1,0:T(8,128)(2,1)} %copy.8.w3_ref), custom_call_target="tpu_custom_call" | custom-call | tf_op jit(solution)/shard_map/pallas_call | solution.py:303
  142.9 74.7 %shard_map.66 = bf16[256,2048]{1,0:T(8,128)(2,1)} custom-call(f32[4,16,256]{2,1,0:T(8,128)} %get-tuple-element.7.rt_ref, bf16[16,192,352]{2,1,0:T(8,128)(2,1)} %shard_map.65.h_ref, bf16[16,352,2048]{2,1,0:T(8,128)(2,1)} %w2_ref.1), custom_call_target="tpu_custom_call" | custom-call | tf_op jit(solution)/shard_map/pallas_call | solution.py:317
  217.5 2.3 %copy.10 = bf16[256,2048]{1,0:T(8,128)(2,1)} copy(bf16[256,2048]{1,0:T(8,128)(2,1)} %shard_map.66) | data formatting | bytes 2097152
  (1 shorter events, 0.0 us)

commit v2 on v0

v2 whole, which is shorter than its diff:
```python
import functools

import jax
import jax.numpy as jnp
from jax import lax
from jax.experimental import pallas as pl
from jax.experimental.pallas import tpu as pltpu
from jax.sharding import PartitionSpec as P

MESH = pl.DeviceIdType.MESH
CF = 2
BF = jnp.bfloat16
F32 = jnp.float32
VMEM_LIMIT = 64 * 1000 * 1000


def _peers():
    z, t = lax.axis_index("ep"), lax.axis_index("tp")
    zs = (3 - z, lax.rem(z + 2, 4), z + 1 - 2 * lax.rem(z, 2))
    yq = lax.rem(t + 2, 4)
    cq = t + 1 - 2 * lax.rem(t, 2)
    return z, t, zs, yq, cq


def _entry_barrier(zs, yq, cq):
    bar = pltpu.get_barrier_semaphore()
    for p in zs:
        pl.semaphore_signal(bar, inc=1, device_id={"ep": p}, device_id_type=MESH)
    for p in (yq, cq):
        pl.semaphore_signal(bar, inc=1, device_id={"tp": p}, device_id_type=MESH)
    pl.semaphore_wait(bar, 5)


def _rcopy(src, dst, ss, rs, dev):
    return pltpu.make_async_remote_copy(
        src_ref=src, dst_ref=dst, send_sem=ss, recv_sem=rs, device_id=dev, device_id_type=MESH
    )


def _members(rt, el, ebase, k):
    tl = rt.shape[1]
    eid = lax.broadcasted_iota(jnp.int32, (el, tl), 0) + ebase
    m = jnp.zeros((el, tl), F32)
    gm = jnp.zeros((el, tl), F32)
    for j in range(k):
        hit = rt[j : j + 1, :].astype(jnp.int32) == eid
        m = jnp.where(hit, 1.0, m)
        gm = jnp.where(hit, rt[8 + j : 9 + j, :], gm)
    a = lax.broadcasted_iota(jnp.int32, (tl, tl), 0)
    b = lax.broadcasted_iota(jnp.int32, (tl, tl), 1)
    u = jnp.where(a < b, 1.0, 0.0).astype(BF)
    slot = jnp.dot(m.astype(BF), u, preferred_element_type=F32)
    return jnp.where(m > 0, slot, -1.0), gm


NB = 256
UN = 256
EB = 4
SL = 4
NT = (((1,), (1,)), ((), ()))


def _moe_kernel(
    k, cap, x_ref, id_ref, g_ref, w1_ref, w3_ref, w2_ref, y_ref,
    xb, rb, pm, gt, xe, hacc, hb, wb, w2b, ypb, part, drecv, yrecv, zrecv, yb,
    lsem, rsem, xsem, wsem, w2sem, dsem, ysem, zsem, zrsem, fsem,
):
    z, t, zs, yq, cq = _peers()
    ns, tl, d = xb.shape
    el, fl = hb.shape[0], hb.shape[2]
    ebase = z * el
    nr = tl // 4
    nu = d // UN
    ng = el // EB
    side = z // 2
    inner = (z == 1) | (z == 2)

    def wcopies(step):
        c, g = step // ng, lax.rem(step, ng)
        sl = lax.rem(step, SL)
        cs = pl.ds(pl.multiple_of(c * UN, UN), UN)
        es = pl.ds(g * EB, EB)
        return (
            pltpu.make_async_copy(w1_ref.at[es, :, cs], wb.at[sl, :, pl.ds(0, fl)], wsem.at[0, sl]),
            pltpu.make_async_copy(w3_ref.at[es, :, cs], wb.at[sl, :, pl.ds(fl, fl)], wsem.at[1, sl]),
        )

    def wstart(step):
        for c in wcopies(step):
            c.start()

    own4 = (lax.rem(cq + 2, 4), yq, cq, t)
    cols = [own4[kd] * 512 + n * NB for n in range(2) for kd in range(4)]

    def w2copy(b):
        return pltpu.make_async_copy(
            w2_ref.at[:, :, pl.ds(pl.multiple_of(cols[b], NB), NB)], w2b.at[b % 2], w2sem.at[b % 2]
        )

    own = pltpu.make_async_copy(x_ref, xb.at[z], lsem.at[0])
    own.start()
    rb[z, 0:k] = id_ref[...].astype(F32)
    rb[z, 8 : 8 + k] = g_ref[...]
    for step in range(SL - 1):
        wstart(step)
    _entry_barrier(zs, yq, cq)
    own.wait()

    def piece(c, s, q):
        return xb.at[s, pl.ds(pl.multiple_of(q * nr, nr), nr), pl.ds(pl.multiple_of(c * UN, UN), UN)]

    def xcopy(kind, c, i):
        p = zs[i]
        if kind == 0:
            r, dev = piece(c, z, t), {"ep": p}
        elif kind == 1:
            r, dev = piece(c, p, t), {"tp": yq}
        elif kind == 2:
            r, dev = piece(c, p, t), {"tp": cq}
        else:
            r, dev = piece(c, p, yq), {"tp": cq}
        return _rcopy(r, r, xsem.at[2 * kind, c, i], xsem.at[2 * kind + 1, c, i], dev)

    def rcopy(i):
        return _rcopy(rb.at[z], rb.at[z], rsem.at[0, i], rsem.at[1, i], {"ep": zs[i]})

    for i in range(3):
        rcopy(i).start()

    @pl.loop(0, nu)
    def _(c):
        for i in range(3):
            xcopy(0, c, i).start()

    def zforward(c):
        for i in range(3):
            xcopy(0, c, i).wait_recv()
            xcopy(1, c, i).start()
            xcopy(2, c, i).start()

    def yforward(c):
        for i in range(3):
            xcopy(1, c, i).wait_recv()
            xcopy(3, c, i).start()

    def xarrive(c):
        for i in range(3):
            xcopy(2, c, i).wait_recv()
            xcopy(3, c, i).wait_recv()

    ci = lax.broadcasted_iota(jnp.int32, (cap, tl), 0).astype(F32)

    def tables(s):
        slot, gm = _members(rb[s], el, ebase, k)
        gs = []
        for i in range(el):
            hit = slot[i : i + 1, :] == ci
            pm[s, i * cap : (i + 1) * cap, :] = jnp.where(hit, 1.0, 0.0).astype(BF)
            gs.append(jnp.where(hit, gm[i : i + 1, :], 0.0))
        g = jnp.concatenate(gs, axis=0).T
        hi = g.astype(BF)
        r = g - hi.astype(F32)
        mid = r.astype(BF)
        gt[s, 0] = hi
        gt[s, 1] = mid
        gt[s, 2] = (r - mid.astype(F32)).astype(BF)

    @pl.loop(0, el)
    def _(e):
        hacc[e] = jnp.zeros(hacc.shape[1:], F32)

    zforward(0)
    for i in range(3):
        rcopy(i).wait_recv()

    @pl.loop(0, 2)
    def _(s):
        tables(s)

    zforward(1)

    @pl.loop(2, 4)
    def _(s):
        tables(s)

    yforward(0)

    @pl.loop(0, nu)
    def _(c):
        @pl.when(c < nu - 2)
        def _():
            zforward(c + 2)

        @pl.when(c < nu - 1)
        def _():
            yforward(c + 1)

        xarrive(c)
        cs = pl.ds(pl.multiple_of(c * UN, UN), UN)

        @pl.loop(0, ns)
        def _(s):
            v = jnp.dot(pm[s], xb[s, :, cs], preferred_element_type=F32).astype(BF)
            xe[:, pl.ds(pl.multiple_of(s * cap, cap), cap), :] = v.reshape(el, cap, UN)

        @pl.loop(0, ng)
        def _(g):
            step = c * ng + g
            for w in wcopies(step):
                w.wait()

            @pl.when(step + SL - 1 < nu * ng)
            def _():
                wstart(step + SL - 1)

            sl = lax.rem(step, SL)
            for i in range(EB):
                e = g * EB + i
                hacc[e] += lax.dot_general(xe[e], wb[sl, i], NT, preferred_element_type=F32)

    w2copy(0).start()

    @pl.loop(0, el)
    def _(e):
        ab = hacc[e]
        hb[e] = (jax.nn.silu(ab[:, :fl]) * ab[:, fl:]).astype(BF)

    def sof(i):
        far = (3 - i) * (1 - side) + i * side
        near = (i - 2) * z + (3 - i) * (1 - z + 4 * side)
        return far * (1 - i // 2) + near * (i // 2)

    def dcopy(n, j, i):
        s = sof(i)
        return _rcopy(
            part.at[n * 4 + 2 * j, s], drecv.at[n, j, s], dsem.at[0, n, j, i], dsem.at[1, n, j, i], {"tp": cq}
        )

    def ycopy(n, i):
        s = sof(i)
        return _rcopy(part.at[n * 4 + 1, s], yrecv.at[n, s], ysem.at[0, n, i], ysem.at[1, n, i], {"tp": yq})

    def compute(n, kd):
        b = n * 4 + kd
        w2copy(b).wait()
        if b + 1 < 8:
            w2copy(b + 1).start()
        sl = b % 2

        @pl.loop(0, el, step=EB)
        def _(e0):
            for i in range(EB):
                e = e0 + i
                v = jnp.dot(hb[e], w2b[sl, e], preferred_element_type=F32).astype(BF)
                ypb[:, pl.ds(pl.multiple_of(e * cap, cap), cap), :] = v.reshape(ns, cap, NB)

        @pl.loop(0, ns)
        def _(i):
            s = sof(i)
            yp = ypb[s]
            acc = jnp.dot(gt[s, 0], yp, preferred_element_type=F32)
            acc += jnp.dot(gt[s, 1], yp, preferred_element_type=F32)
            acc += jnp.dot(gt[s, 2], yp, preferred_element_type=F32)
            if kd % 2 == 0:
                part[b, s] = acc
                dcopy(n, kd // 2, i).start()
            else:
                dcopy(n, kd // 2, i).wait_recv()
                part[b, s] = acc + drecv[n, kd // 2, s]
                if kd == 1:

                    @pl.when(i < 3)
                    def _():
                        ycopy(n, i).start()

    def zcopy(n, i):
        s = sof(i)
        if i < 2:
            dr = side
        else:
            dr = lax.rem(z, 2)
        return _rcopy(
            part.at[n * 4 + 3, s], zrecv.at[n, dr * 4 + s], zsem.at[n, i], zrsem.at[n, dr * 4 + s], {"ep": z + 1 - 2 * dr}
        ), zrecv.at[n, dr * 4 + s]

    def zacc(n, i):
        s = sof(i)
        ycopy(n, i).wait_recv()
        part[n * 4 + 3, s] += yrecv[n, s]
        if i < 3:

            @pl.when(~inner)
            def _():
                zcopy(n, i)[0].start()

    def relay(n, i):
        @pl.when(inner)
        def _():
            c, buf = zcopy(n, i)
            c.wait_recv()
            part[n * 4 + 3, sof(i)] += buf[...]
            c.start()

    def zarrive(n, dr):
        _rcopy(
            part.at[n * 4 + 3, z], zrecv.at[n, dr * 4 + z], zsem.at[n, 0], zrsem.at[n, dr * 4 + z], {"ep": zs[0]}
        ).wait_recv()
        part[n * 4 + 3, z] += zrecv[n, dr * 4 + z]

    def fcopy(j, n):
        q, dev = ((t, yq), (t, cq), (yq, cq))[j]
        sl = pl.ds(pl.multiple_of(q * 512 + n * NB, NB), NB)
        return _rcopy(yb.at[:, sl], yb.at[:, sl], fsem.at[0, n, j], fsem.at[1, n, j], {"tp": dev})

    def finish(n):
        @pl.when(z > 0)
        def _():
            zarrive(n, 0)

        @pl.when(z < 3)
        def _():
            zarrive(n, 1)

        yb[:, pl.ds(pl.multiple_of(t * 512 + n * NB, NB), NB)] = part[n * 4 + 3, z].astype(BF)

    def spread(n):
        fcopy(0, n).start()
        fcopy(1, n).start()

    compute(0, 0)
    compute(0, 1)
    compute(0, 2)
    compute(0, 3)
    zacc(0, 0)
    compute(1, 0)
    zacc(0, 1)
    compute(1, 1)
    ycopy(0, 3).start()
    ycopy(1, 3).start()
    relay(0, 0)
    compute(1, 2)
    zacc(0, 2)
    compute(1, 3)
    relay(0, 1)
    zacc(1, 0)
    relay(0, 2)
    zacc(1, 1)
    relay(1, 0)
    zacc(1, 2)
    relay(1, 1)
    zacc(0, 3)
    relay(1, 2)
    finish(0)
    spread(0)
    zacc(1, 3)
    finish(1)
    spread(1)
    for n in range(2):
        fcopy(0, n).wait_recv()
        fcopy(2, n).start()

    @pl.loop(0, nu)
    def _(c):
        for kind in range(4):
            for i in range(3):
                xcopy(kind, c, i).wait_send()

    for i in range(3):
        rcopy(i).wait_send()
    for n in range(2):
        for i in range(4):
            for j in range(2):
                dcopy(n, j, i).wait_send()
            ycopy(n, i).wait_send()
            if i < 3:
                zcopy(n, i)[0].wait_send()
    for n in range(2):
        fcopy(1, n).wait_recv()
        fcopy(2, n).wait_recv()
    for n in range(2):
        for j in range(3):
            fcopy(j, n).wait_send()
    y_ref[...] = yb[...]


def solution(mesh):
    tok = P(("dp", "ep"), None)
    nep = mesh.shape["ep"]

    def body(x, idx, g, w1, w3, w2):
        tl, d = x.shape
        k = idx.shape[1]
        el, _, fl = w1.shape
        cap = CF * k * tl // (el * nep)
        vm = pl.BlockSpec(memory_space=pltpu.VMEM)
        hbm = pl.BlockSpec(memory_space=pl.ANY)
        dma = pltpu.SemaphoreType.DMA
        nu = d // UN
        return pl.pallas_call(
            functools.partial(_moe_kernel, k, cap),
            out_shape=jax.ShapeDtypeStruct((tl, d), BF),
            in_specs=[hbm, vm, vm, hbm, hbm, hbm],
            out_specs=vm,
            scratch_shapes=[
                pltpu.VMEM((nep, tl, d), BF),
                pltpu.VMEM((nep, 16, tl), F32),
                pltpu.VMEM((nep, el * cap, tl), BF),
                pltpu.VMEM((nep, 3, tl, el * cap), BF),
                pltpu.VMEM((el, nep * cap, UN), BF),
                pltpu.VMEM((el, nep * cap, 2 * fl), F32),
                pltpu.VMEM((el, nep * cap, fl), BF),
                pltpu.VMEM((SL, EB, 2 * fl, UN), BF),
                pltpu.VMEM((2, el, fl, NB), BF),
                pltpu.VMEM((nep, el * cap, NB), BF),
                pltpu.VMEM((8, nep, tl, NB), F32),
                pltpu.VMEM((2, 2, nep, tl, NB), F32),
                pltpu.VMEM((2, nep, tl, NB), F32),
                pltpu.VMEM((2, 8, tl, NB), F32),
                pltpu.VMEM((tl, d), BF),
                dma((1,)),
                dma((2, 3)),
                dma((8, nu, 3)),
                dma((2, SL)),
                dma((2,)),
                dma((2, 2, 2, 4)),
                dma((2, 2, 4)),
                dma((2, 3)),
                dma((2, 8)),
                dma((2, 2, 3)),
            ],
            compiler_params=pltpu.CompilerParams(
                collective_id=0, has_side_effects=True, vmem_limit_bytes=VMEM_LIMIT
            ),
        )(x, idx.T, g.T, w1.swapaxes(1, 2), w3.swapaxes(1, 2), w2)

    return jax.shard_map(
        body,
        mesh=mesh,
        in_specs=(tok, tok, tok, P("ep", None, "tp"), P("ep", None, "tp"), P("ep", "tp", None)),
        out_specs=tok,
        check_vma=False,
    )
```

time: 774 us -> 119 us (0.15)
  blocking collectives: 494 us -> 0 us
  Pallas kernels: 0 us -> 117 us
  local copies, waits for them, and re-layouts: 102 us -> 2.3 us
  waiting for transfers between devices: 80.6 us -> 0 us
  matrix products: 44.5 us -> 0 us
  other arithmetic: 38.5 us -> 0 us
  between operations: 13.5 us -> 0.01 us
    all_to_all x3 -> x0, blocking collectives: 494 us -> none  [the longest x1 279 us: body(): recv = lax.all_to_all(buf.reshape(nep, EL, C, D), 'ep', 0, 0, tiled=True)]
    pallas_call x0 -> x1, Pallas kernels: none -> 117 us  [body(): pl.pallas_call(functools.partial(_moe_kernel, k, cap), out_shape=jax.Shap...]
    all_gather x1 -> x0, waiting for transfers between devices: 80.6 us -> none  [body(): yall = lax.all_gather(back, 'tp', axis=1, tiled=True).reshape(E * C, D)]
    dot_general x2 -> x0, matrix products: 44.5 us -> none  [the longest x1 27.3 us: body(): jnp.einsum('esf,efd->esd', h, w2, preferred_element_type=jnp.float32)]
    gather x2 -> x0, local copies, waits for them, and re-layouts: 29.9 us -> none  [body(): jnp.take(yall, dest, axis=0, mode='fill', fill_value=0).reshape(TL, K, D)]
    reduce_sum x3 -> x0, other arithmetic: 19.9 us -> none  [the longest x1 11.4 us: body(): out = jnp.sum(yc.astype(jnp.float32) * g[:, :, None], axis=1)]
    another operation x3 -> x0, other arithmetic: 18.4 us -> none
    scatter x1 -> x0, local copies, waits for them, and re-layouts: 17.4 us -> none  [body(): jnp.zeros((E * C, D), x.dtype).at[dest]]
  transfers between devices with their start and end apart: 1 -> 0, of which waited for: 1 -> 0; matrix products, arithmetic and copies ran while one was open for 0% -> 0% of each run, Pallas kernels for 0% -> 0%
where the time goes in v2:
time: 119 us
  Pallas kernels  117 us (98%)
  local copies, waits for them, and re-layouts  2.3 us (2%)
    pallas_call x1, Pallas kernels, body(): pl.pallas_call(functools.partial(_moe_kernel, k, cap), out_shape=jax.Shap...  117 us

profile of v2, /device:TPU:0, one launch (start us, length us, event | category | flops | bytes accessed | tf_op | source)
XLA Modules:
  0.0 118.9 jit_solution(3113439154405144626)
XLA Ops:
  0.0 116.6 %shard_map.64 = bf16[256,2048]{1,0:T(8,128)(2,1)} custom-call(bf16[256,2048]{1,0:T(8,128)(2,1)} %x_ref.1, s32[6,256]{1,0:T(8,128)} %bitcast.6, f32[6,256]{1,0:T(8,128)} %bitcast.7, bf16[16,352,2048]{2,1,0:T(8,128)(2,1)} %bitcast.4, bf16[16,352,2048]{2,1,0:T(8,128)(2,1)} %bitcast.5, bf16[16,352,2048]{2,1,0:T(8,128)(2,1)} %w2_ref.1), custom_call_target="tpu_custom_call" | custom-call | tf_op jit(solution)/shard_map/pallas_call | solution.py:399
  116.6 2.3 %copy.8 = bf16[256,2048]{1,0:T(8,128)(2,1)} copy(bf16[256,2048]{1,0:T(8,128)(2,1)} %shard_map.64) | data formatting | bytes 2097152

commit v3 on v2

--- a/solution.py
+++ b/solution.py
@@ -55,15 +55,16 @@
 
 NB = 256
 UN = 256
+CU = 512
 EB = 4
-SL = 4
+SL = 3
 NT = (((1,), (1,)), ((), ()))
 
 
 def _moe_kernel(
     k, cap, x_ref, id_ref, g_ref, w1_ref, w3_ref, w2_ref, y_ref,
-    xb, rb, pm, gt, xe, hacc, hb, wb, w2b, ypb, part, drecv, yrecv, zrecv, yb,
-    lsem, rsem, xsem, wsem, w2sem, dsem, ysem, zsem, zrsem, fsem,
+    xb, rb, pm, gt, xe, hacc, hb, wb, w2b, part, drecv, yrecv, zrecv, zfrecv, yb,
+    lsem, rsem, xsem, wsem, w2sem, dsem, ysem, zsem, zrsem, zfsem, fsem,
 ):
     z, t, zs, yq, cq = _peers()
     ns, tl, d = xb.shape
@@ -71,6 +72,7 @@
     ebase = z * el
     nr = tl // 4
     nu = d // UN
+    nc = d // CU
     ng = el // EB
     side = z // 2
     inner = (z == 1) | (z == 2)
@@ -78,7 +80,7 @@
     def wcopies(step):
         c, g = step // ng, lax.rem(step, ng)
         sl = lax.rem(step, SL)
-        cs = pl.ds(pl.multiple_of(c * UN, UN), UN)
+        cs = pl.ds(pl.multiple_of(c * CU, CU), CU)
         es = pl.ds(g * EB, EB)
         return (
             pltpu.make_async_copy(w1_ref.at[es, :, cs], wb.at[sl, :, pl.ds(0, fl)], wsem.at[0, sl]),
@@ -103,6 +105,8 @@
     rb[z, 8 : 8 + k] = g_ref[...]
     for step in range(SL - 1):
         wstart(step)
+    w2copy(0).start()
+    w2copy(1).start()
     _entry_barrier(zs, yq, cq)
     own.wait()
 
@@ -183,47 +187,61 @@
     def _(s):
         tables(s)
 
+    zforward(2)
     yforward(0)
-
-    @pl.loop(0, nu)
+    yforward(1)
+    zforward(3)
+
+    @pl.loop(0, nc)
     def _(c):
-        @pl.when(c < nu - 2)
-        def _():
-            zforward(c + 2)
-
-        @pl.when(c < nu - 1)
-        def _():
-            yforward(c + 1)
-
-        xarrive(c)
-        cs = pl.ds(pl.multiple_of(c * UN, UN), UN)
-
-        @pl.loop(0, ns)
-        def _(s):
+        u = c * (CU // UN)
+        xarrive(u)
+        xarrive(u + 1)
+        cs = pl.ds(pl.multiple_of(c * CU, CU), CU)
+        for s in range(ns):
             v = jnp.dot(pm[s], xb[s, :, cs], preferred_element_type=F32).astype(BF)
-            xe[:, pl.ds(pl.multiple_of(s * cap, cap), cap), :] = v.reshape(el, cap, UN)
-
-        @pl.loop(0, ng)
-        def _(g):
+            xe[:, s * cap : (s + 1) * cap, :] = v.reshape(el, cap, CU)
+        for g in range(ng):
             step = c * ng + g
+            if g == 1:
+
+                @pl.when(c < nc - 1)
+                def _():
+                    yforward(u + 2)
+
+            if g == 2:
+
+                @pl.when(c < nc - 2)
+                def _():
+                    zforward(u + 4)
+
+            if g == 3:
+
+                @pl.when(c < nc - 1)
+                def _():
+                    yforward(u + 3)
+
             for w in wcopies(step):
                 w.wait()
 
-            @pl.when(step + SL - 1 < nu * ng)
+            @pl.when(step + SL - 1 < nc * ng)
             def _():
                 wstart(step + SL - 1)
 
             sl = lax.rem(step, SL)
             for i in range(EB):
                 e = g * EB + i
-                hacc[e] += lax.dot_general(xe[e], wb[sl, i], NT, preferred_element_type=F32)
-
-    w2copy(0).start()
-
-    @pl.loop(0, el)
-    def _(e):
-        ab = hacc[e]
-        hb[e] = (jax.nn.silu(ab[:, :fl]) * ab[:, fl:]).astype(BF)
+                hacc[e] += lax.dot_general(wb[sl, i], xe[e], NT, preferred_element_type=F32)
+
+        @pl.when(c < nc - 2)
+        def _():
+            zforward(u + 5)
+
+    @pl.loop(0, el, step=2)
+    def _(e0):
+        for i in range(2):
+            ab = hacc[e0 + i]
+            hb[e0 + i] = (jax.nn.silu(ab[:fl]) * ab[fl:]).T.astype(BF)
 
     def sof(i):
         far = (3 - i) * (1 - side) + i * side
@@ -240,24 +258,28 @@
         s = sof(i)
         return _rcopy(part.at[n * 4 + 1, s], yrecv.at[n, s], ysem.at[0, n, i], ysem.at[1, n, i], {"tp": yq})
 
+    def zfirst():
+        return _rcopy(part.at[1, sof(2)], zfrecv, zfsem.at[0], zfsem.at[1], {"ep": zs[2]})
+
     def compute(n, kd):
         b = n * 4 + kd
         w2copy(b).wait()
-        if b + 1 < 8:
-            w2copy(b + 1).start()
         sl = b % 2
 
-        @pl.loop(0, el, step=EB)
+        @pl.loop(0, el, step=8)
         def _(e0):
-            for i in range(EB):
+            for i in range(8):
                 e = e0 + i
                 v = jnp.dot(hb[e], w2b[sl, e], preferred_element_type=F32).astype(BF)
-                ypb[:, pl.ds(pl.multiple_of(e * cap, cap), cap), :] = v.reshape(ns, cap, NB)
+                pm[:, pl.ds(pl.multiple_of(e * cap, cap), cap), :] = v.reshape(ns, cap, NB)
+
+        if b + 2 < 8:
+            w2copy(b + 2).start()
 
         @pl.loop(0, ns)
         def _(i):
             s = sof(i)
-            yp = ypb[s]
+            yp = pm[s]
             acc = jnp.dot(gt[s, 0], yp, preferred_element_type=F32)
             acc += jnp.dot(gt[s, 1], yp, preferred_element_type=F32)
             acc += jnp.dot(gt[s, 2], yp, preferred_element_type=F32)
@@ -269,43 +291,48 @@
                 part[b, s] = acc + drecv[n, kd // 2, s]
                 if kd == 1:
 
-                    @pl.when(i < 3)
+                    @pl.when(i < 2 + n)
                     def _():
                         ycopy(n, i).start()
 
+                    if n == 0:
+
+                        @pl.when(i == 2)
+                        def _():
+                            zfirst().start()
+
+    def zdir(i):
+        return side if i < 2 else lax.rem(z, 2)
+
     def zcopy(n, i):
-        s = sof(i)
-        if i < 2:
-            dr = side
-        else:
-            dr = lax.rem(z, 2)
-        return _rcopy(
-            part.at[n * 4 + 3, s], zrecv.at[n, dr * 4 + s], zsem.at[n, i], zrsem.at[n, dr * 4 + s], {"ep": z + 1 - 2 * dr}
-        ), zrecv.at[n, dr * 4 + s]
+        s, dr = sof(i), zdir(i)
+        dn = z + 1 - 2 * dr
+        slot = s - dn + 4 * dr
+        return _rcopy(part.at[n * 4 + 3, s], zrecv.at[n, slot], zsem.at[n, i], zrsem.at[n, slot], {"ep": dn})
+
+    def zarrive(n, s, slot):
+        _rcopy(
+            part.at[n * 4 + 3, s], zrecv.at[n, slot], zsem.at[n, 0], zrsem.at[n, slot], {"ep": zs[0]}
+        ).wait_recv()
+        part[n * 4 + 3, s] += zrecv[n, slot]
 
     def zacc(n, i):
         s = sof(i)
-        ycopy(n, i).wait_recv()
-        part[n * 4 + 3, s] += yrecv[n, s]
+        if (n, i) != (0, 2):
+            ycopy(n, i).wait_recv()
+            part[n * 4 + 3, s] += yrecv[n, s]
         if i < 3:
 
             @pl.when(~inner)
             def _():
-                zcopy(n, i)[0].start()
+                zcopy(n, i).start()
 
     def relay(n, i):
         @pl.when(inner)
         def _():
-            c, buf = zcopy(n, i)
-            c.wait_recv()
-            part[n * 4 + 3, sof(i)] += buf[...]
-            c.start()
-
-    def zarrive(n, dr):
-        _rcopy(
-            part.at[n * 4 + 3, z], zrecv.at[n, dr * 4 + z], zsem.at[n, 0], zrsem.at[n, dr * 4 + z], {"ep": zs[0]}
-        ).wait_recv()
-        part[n * 4 + 3, z] += zrecv[n, dr * 4 + z]
+            s = sof(i)
+            zarrive(n, s, s - z + 4 * zdir(i))
+            zcopy(n, i).start()
 
     def fcopy(j, n):
         q, dev = ((t, yq), (t, cq), (yq, cq))[j]
@@ -315,11 +342,11 @@
     def finish(n):
         @pl.when(z > 0)
         def _():
-            zarrive(n, 0)
+            zarrive(n, z, 0)
 
         @pl.when(z < 3)
         def _():
-            zarrive(n, 1)
+            zarrive(n, z, 4)
 
         yb[:, pl.ds(pl.multiple_of(t * 512 + n * NB, NB), NB)] = part[n * 4 + 3, z].astype(BF)
 
@@ -331,20 +358,22 @@
     compute(0, 1)
     compute(0, 2)
     compute(0, 3)
+    zacc(0, 2)
     zacc(0, 0)
     compute(1, 0)
     zacc(0, 1)
     compute(1, 1)
+    zfirst().wait_recv()
+    part[1, z] += zfrecv[...]
     ycopy(0, 3).start()
     ycopy(1, 3).start()
     relay(0, 0)
     compute(1, 2)
-    zacc(0, 2)
     compute(1, 3)
     relay(0, 1)
     zacc(1, 0)
+    zacc(1, 1)
     relay(0, 2)
-    zacc(1, 1)
     relay(1, 0)
     zacc(1, 2)
     relay(1, 1)
@@ -371,16 +400,20 @@
         for i in range(4):
             for j in range(2):
                 dcopy(n, j, i).wait_send()
-            ycopy(n, i).wait_send()
+            if (n, i) != (0, 2):
+                ycopy(n, i).wait_send()
             if i < 3:
-                zcopy(n, i)[0].wait_send()
+                zcopy(n, i).wait_send()
+    zfirst().wait_send()
     for n in range(2):
         fcopy(1, n).wait_recv()
         fcopy(2, n).wait_recv()
     for n in range(2):
         for j in range(3):
             fcopy(j, n).wait_send()
-    y_ref[...] = yb[...]
+    out = pltpu.make_async_copy(yb, y_ref, lsem.at[0])
+    out.start()
+    out.wait()
 
 
 def solution(mesh):
@@ -400,22 +433,22 @@
             functools.partial(_moe_kernel, k, cap),
             out_shape=jax.ShapeDtypeStruct((tl, d), BF),
             in_specs=[hbm, vm, vm, hbm, hbm, hbm],
-            out_specs=vm,
+            out_specs=hbm,
             scratch_shapes=[
                 pltpu.VMEM((nep, tl, d), BF),
                 pltpu.VMEM((nep, 16, tl), F32),
                 pltpu.VMEM((nep, el * cap, tl), BF),
                 pltpu.VMEM((nep, 3, tl, el * cap), BF),
-                pltpu.VMEM((el, nep * cap, UN), BF),
-                pltpu.VMEM((el, nep * cap, 2 * fl), F32),
+                pltpu.VMEM((el, nep * cap, CU), BF),
+                pltpu.VMEM((el, 2 * fl, nep * cap), F32),
                 pltpu.VMEM((el, nep * cap, fl), BF),
-                pltpu.VMEM((SL, EB, 2 * fl, UN), BF),
+                pltpu.VMEM((SL, EB, 2 * fl, CU), BF),
                 pltpu.VMEM((2, el, fl, NB), BF),
-                pltpu.VMEM((nep, el * cap, NB), BF),
                 pltpu.VMEM((8, nep, tl, NB), F32),
                 pltpu.VMEM((2, 2, nep, tl, NB), F32),
                 pltpu.VMEM((2, nep, tl, NB), F32),
-                pltpu.VMEM((2, 8, tl, NB), F32),
+                pltpu.VMEM((2, 5, tl, NB), F32),
+                pltpu.VMEM((tl, NB), F32),
                 pltpu.VMEM((tl, d), BF),
                 dma((1,)),
                 dma((2, 3)),
@@ -425,7 +458,8 @@
                 dma((2, 2, 2, 4)),
                 dma((2, 2, 4)),
                 dma((2, 3)),
-                dma((2, 8)),
+                dma((2, 5)),
+                dma((2,)),
                 dma((2, 2, 3)),
             ],
             compiler_params=pltpu.CompilerParams(

time: 119 us -> 111 us (0.933)
  Pallas kernels: 117 us -> 109 us
    pallas_call x1, Pallas kernels: 117 us -> 109 us  [body(): pl.pallas_call(functools.partial(_moe_kernel, k, cap), out_shape=jax.Shap...]
where the time goes in v3:
time: 111 us
  Pallas kernels  109 us (98%)
  local copies, waits for them, and re-layouts  2.3 us (2%)
    pallas_call x1, Pallas kernels, body(): pl.pallas_call(functools.partial(_moe_kernel, k, cap), out_shape=jax.Shap...  109 us
    unnamed x1, local copies, waits for them, and re-layouts  2.3 us

profile of v3, /device:TPU:0, one launch (start us, length us, event | category | flops | bytes accessed | tf_op | source)
XLA Modules:
  0.0 111.2 jit_solution(2560926653394301031)
XLA Ops:
  0.0 108.9 %shard_map.64 = bf16[256,2048]{1,0:T(8,128)(2,1)} custom-call(bf16[256,2048]{1,0:T(8,128)(2,1)} %x_ref.1, s32[6,256]{1,0:T(8,128)} %bitcast.6, f32[6,256]{1,0:T(8,128)} %bitcast.7, bf16[16,352,2048]{2,1,0:T(8,128)(2,1)} %bitcast.4, bf16[16,352,2048]{2,1,0:T(8,128)(2,1)} %bitcast.5, bf16[16,352,2048]{2,1,0:T(8,128)(2,1)} %w2_ref.1), custom_call_target="tpu_custom_call" | custom-call | tf_op jit(solution)/shard_map/pallas_call | solution.py:432
  108.9 2.3 %copy.8 = bf16[256,2048]{1,0:T(8,128)(2,1)} copy(bf16[256,2048]{1,0:T(8,128)(2,1)} %shard_map.64) | data formatting | bytes 2097152

commit v4 on v3

--- a/solution.py
+++ b/solution.py
@@ -22,13 +22,19 @@
     return z, t, zs, yq, cq
 
 
-def _entry_barrier(zs, yq, cq):
+def _entry_barrier(inner, zs, yq, cq):
     bar = pltpu.get_barrier_semaphore()
-    for p in zs:
+
+    @pl.when(inner)
+    def _():
+        pl.semaphore_signal(bar, inc=1, device_id={"ep": zs[0]}, device_id_type=MESH)
+
+    for p in zs[1:]:
         pl.semaphore_signal(bar, inc=1, device_id={"ep": p}, device_id_type=MESH)
     for p in (yq, cq):
         pl.semaphore_signal(bar, inc=1, device_id={"tp": p}, device_id_type=MESH)
-    pl.semaphore_wait(bar, 5)
+    z = lax.axis_index("ep")
+    pl.semaphore_wait(bar, 4 + z * (3 - z) // 2)
 
 
 def _rcopy(src, dst, ss, rs, dev):
@@ -56,15 +62,26 @@
 NB = 256
 UN = 256
 CU = 512
+FWD = {
+    (0, 1): ((0, 4), (1, 1), (2, 3)),
+    (0, 3): ((0, 5), (1, 2), (2, 4)),
+    (1, 1): ((0, 6), (1, 3), (2, 5)),
+    (1, 3): ((0, 7), (1, 4), (2, 6)),
+    (2, 0): ((1, 5), (2, 7)),
+    (2, 2): ((1, 6),),
+    (3, 0): ((1, 7),),
+}
+UNITS = ((0, 1), (1, 2), (3, 2), (5, 2), (7, 1))
+HR = 64
 EB = 4
-SL = 3
+SL = 4
 NT = (((1,), (1,)), ((), ()))
 
 
 def _moe_kernel(
     k, cap, x_ref, id_ref, g_ref, w1_ref, w3_ref, w2_ref, y_ref,
-    xb, rb, pm, gt, xe, hacc, hb, wb, w2b, part, drecv, yrecv, zrecv, zfrecv, yb,
-    lsem, rsem, xsem, wsem, w2sem, dsem, ysem, zsem, zrsem, zfsem, fsem,
+    xb, rb, pm, gt, xe, hp, hb, wb, w2b, drecv, yrecv, zrecv, zfrecv, yb,
+    lsem, rsem, xsem, xfsem, wsem, w2sem, dsem, ysem, zsem, zrsem, zfsem, fsem, hsem,
 ):
     z, t, zs, yq, cq = _peers()
     ns, tl, d = xb.shape
@@ -72,19 +89,27 @@
     ebase = z * el
     nr = tl // 4
     nu = d // UN
-    nc = d // CU
     ng = el // EB
     side = z // 2
     inner = (z == 1) | (z == 2)
 
+    def hacc(e):
+        return hp.at[pl.ds(pl.multiple_of(e * 2 * fl, 2 * fl), 2 * fl), pl.ds(0, ns * cap)]
+
+    def part(b, s):
+        return hp.at[pl.ds(pl.multiple_of((b * ns + s) * tl, tl), tl), :]
+
+    wsteps = [(j, g) for j in range(len(UNITS)) for g in range(ng)]
+
     def wcopies(step):
-        c, g = step // ng, lax.rem(step, ng)
-        sl = lax.rem(step, SL)
-        cs = pl.ds(pl.multiple_of(c * CU, CU), CU)
+        j, g = wsteps[step]
+        u0, n = UNITS[j]
+        sl = step % SL
+        cs, ws = pl.ds(u0 * UN, n * UN), pl.ds(0, n * UN)
         es = pl.ds(g * EB, EB)
         return (
-            pltpu.make_async_copy(w1_ref.at[es, :, cs], wb.at[sl, :, pl.ds(0, fl)], wsem.at[0, sl]),
-            pltpu.make_async_copy(w3_ref.at[es, :, cs], wb.at[sl, :, pl.ds(fl, fl)], wsem.at[1, sl]),
+            pltpu.make_async_copy(w1_ref.at[es, :, cs], wb.at[sl, :, pl.ds(0, fl), ws], wsem.at[0, sl]),
+            pltpu.make_async_copy(w3_ref.at[es, :, cs], wb.at[sl, :, pl.ds(fl, fl), ws], wsem.at[1, sl]),
         )
 
     def wstart(step):
@@ -107,7 +132,7 @@
         wstart(step)
     w2copy(0).start()
     w2copy(1).start()
-    _entry_barrier(zs, yq, cq)
+    _entry_barrier(inner, zs, yq, cq)
     own.wait()
 
     def piece(c, s, q):
@@ -128,22 +153,54 @@
     def rcopy(i):
         return _rcopy(rb.at[z], rb.at[z], rsem.at[0, i], rsem.at[1, i], {"ep": zs[i]})
 
-    for i in range(3):
-        rcopy(i).start()
-
-    @pl.loop(0, nu)
+    def xpass(c):
+        r = piece(c, zs[1], t)
+        return _rcopy(r, r, xfsem.at[c], xsem.at[1, c, 0], {"ep": zs[2]})
+
+    def rpass():
+        return _rcopy(rb.at[zs[1]], rb.at[zs[1]], rsem.at[0, 3], rsem.at[1, 0], {"ep": zs[2]})
+
+    rcopy(1).start()
+    xcopy(0, 0, 1).start()
+
+    @pl.when(inner)
+    def _():
+        rcopy(0).start()
+        xcopy(0, 0, 0).start()
+
+    rcopy(2).start()
+    xcopy(0, 0, 2).start()
+
+    @pl.loop(1, nu)
     def _(c):
-        for i in range(3):
-            xcopy(0, c, i).start()
-
-    def zforward(c):
-        for i in range(3):
-            xcopy(0, c, i).wait_recv()
-            xcopy(1, c, i).start()
-            xcopy(2, c, i).start()
+        xcopy(0, c, 1).start()
+
+        @pl.when(inner)
+        def _():
+            xcopy(0, c, 0).start()
+
+        xcopy(0, c, 2).start()
+
+    def zhand(c, i):
+        xcopy(0, c, i).wait_recv()
+        if i == 1:
+
+            @pl.when(inner)
+            def _():
+                xpass(c).start()
+
+        xcopy(1, c, i).start()
+        xcopy(2, c, i).start()
+
+    def zfar(c):
+        zhand(c, 1)
+
+    def znear(c):
+        zhand(c, 2)
+        zhand(c, 0)
 
     def yforward(c):
-        for i in range(3):
+        for i in (1, 2, 0):
             xcopy(1, c, i).wait_recv()
             xcopy(3, c, i).start()
 
@@ -169,79 +226,53 @@
         gt[s, 1] = mid
         gt[s, 2] = (r - mid.astype(F32)).astype(BF)
 
-    @pl.loop(0, el)
-    def _(e):
-        hacc[e] = jnp.zeros(hacc.shape[1:], F32)
-
-    zforward(0)
-    for i in range(3):
-        rcopy(i).wait_recv()
-
-    @pl.loop(0, 2)
-    def _(s):
-        tables(s)
-
-    zforward(1)
-
-    @pl.loop(2, 4)
-    def _(s):
-        tables(s)
-
-    zforward(2)
+    rcopy(1).wait_recv()
+
+    @pl.when(inner)
+    def _():
+        rpass().start()
+
+    zfar(0)
+    rcopy(2).wait_recv()
+    tables(z)
+    zfar(1)
+    znear(0)
+    tables(zs[2])
+    zfar(2)
+    znear(1)
+    rcopy(0).wait_recv()
+    tables(zs[1])
+    zfar(3)
+    tables(zs[0])
     yforward(0)
-    yforward(1)
-    zforward(3)
-
-    @pl.loop(0, nc)
-    def _(c):
-        u = c * (CU // UN)
-        xarrive(u)
-        xarrive(u + 1)
-        cs = pl.ds(pl.multiple_of(c * CU, CU), CU)
+    znear(2)
+
+    for j, (u0, un) in enumerate(UNITS):
+        for u in range(u0, u0 + un):
+            xarrive(u)
+        cs = pl.ds(u0 * UN, un * UN)
         for s in range(ns):
             v = jnp.dot(pm[s], xb[s, :, cs], preferred_element_type=F32).astype(BF)
-            xe[:, s * cap : (s + 1) * cap, :] = v.reshape(el, cap, CU)
+            xe[:, s * cap : (s + 1) * cap, 0 : un * UN] = v.reshape(el, cap, un * UN)
         for g in range(ng):
-            step = c * ng + g
-            if g == 1:
-
-                @pl.when(c < nc - 1)
-                def _():
-                    yforward(u + 2)
-
-            if g == 2:
-
-                @pl.when(c < nc - 2)
-                def _():
-                    zforward(u + 4)
-
-            if g == 3:
-
-                @pl.when(c < nc - 1)
-                def _():
-                    yforward(u + 3)
-
+            step = j * ng + g
+            for f, u in FWD.get((j, g), ()):
+                (zfar, yforward, znear)[f](u)
             for w in wcopies(step):
                 w.wait()
-
-            @pl.when(step + SL - 1 < nc * ng)
-            def _():
+            if step + SL - 1 < len(wsteps):
                 wstart(step + SL - 1)
-
-            sl = lax.rem(step, SL)
             for i in range(EB):
                 e = g * EB + i
-                hacc[e] += lax.dot_general(wb[sl, i], xe[e], NT, preferred_element_type=F32)
-
-        @pl.when(c < nc - 2)
-        def _():
-            zforward(u + 5)
-
-    @pl.loop(0, el, step=2)
-    def _(e0):
-        for i in range(2):
-            ab = hacc[e0 + i]
-            hb[e0 + i] = (jax.nn.silu(ab[:fl]) * ab[fl:]).T.astype(BF)
+                v = lax.dot_general(
+                    wb[step % SL, i, :, 0 : un * UN], xe[e, :, 0 : un * UN], NT, preferred_element_type=F32
+                )
+                if j > 0:
+                    v += hacc(e)[...]
+                if j < len(UNITS) - 1:
+                    hacc(e)[...] = v
+                else:
+                    hb[e] = (jax.nn.silu(v[:fl]) * v[fl:]).T.astype(BF)
 
     def sof(i):
         far = (3 - i) * (1 - side) + i * side
@@ -251,15 +282,15 @@
     def dcopy(n, j, i):
         s = sof(i)
         return _rcopy(
-            part.at[n * 4 + 2 * j, s], drecv.at[n, j, s], dsem.at[0, n, j, i], dsem.at[1, n, j, i], {"tp": cq}
+            part(n * 4 + 2 * j, s), drecv.at[n, j, s], dsem.at[0, n, j, i], dsem.at[1, n, j, i], {"tp": cq}
         )
 
     def ycopy(n, i):
         s = sof(i)
-        return _rcopy(part.at[n * 4 + 1, s], yrecv.at[n, s], ysem.at[0, n, i], ysem.at[1, n, i], {"tp": yq})
+        return _rcopy(part(n * 4 + 1, s), yrecv.at[n, s], ysem.at[0, n, i], ysem.at[1, n, i], {"tp": yq})
 
     def zfirst():
-        return _rcopy(part.at[1, sof(2)], zfrecv, zfsem.at[0], zfsem.at[1], {"ep": zs[2]})
+        return _rcopy(part(1, sof(2)), zfrecv, zfsem.at[0], zfsem.at[1], {"ep": zs[2]})
 
     def compute(n, kd):
         b = n * 4 + kd
@@ -284,11 +315,11 @@
             acc += jnp.dot(gt[s, 1], yp, preferred_element_type=F32)
             acc += jnp.dot(gt[s, 2], yp, preferred_element_type=F32)
             if kd % 2 == 0:
-                part[b, s] = acc
+                part(b, s)[...] = acc
                 dcopy(n, kd // 2, i).start()
             else:
                 dcopy(n, kd // 2, i).wait_recv()
-                part[b, s] = acc + drecv[n, kd // 2, s]
+                part(b, s)[...] = acc + drecv[n, kd // 2, s]
                 if kd == 1:
 
                     @pl.when(i < 2 + n)
@@ -308,19 +339,23 @@
         s, dr = sof(i), zdir(i)
         dn = z + 1 - 2 * dr
         slot = s - dn + 4 * dr
-        return _rcopy(part.at[n * 4 + 3, s], zrecv.at[n, slot], zsem.at[n, i], zrsem.at[n, slot], {"ep": dn})
+        return _rcopy(part(n * 4 + 3, s), zrecv.at[n, slot], zsem.at[n, i], zrsem.at[n, slot], {"ep": dn})
 
     def zarrive(n, s, slot):
         _rcopy(
-            part.at[n * 4 + 3, s], zrecv.at[n, slot], zsem.at[n, 0], zrsem.at[n, slot], {"ep": zs[0]}
+            part(n * 4 + 3, s), zrecv.at[n, slot], zsem.at[n, 0], zrsem.at[n, slot], {"ep": zs[0]}
         ).wait_recv()
-        part[n * 4 + 3, s] += zrecv[n, slot]
+        part(n * 4 + 3, s)[...] += zrecv[n, slot]
+
+    def hcopy(r):
+        rs = pl.ds(r * HR, HR)
+        return _rcopy(part(5, z).at[rs], yrecv.at[1, z, rs], hsem.at[0, r], hsem.at[1, r], {"tp": yq})
 
     def zacc(n, i):
         s = sof(i)
         if (n, i) != (0, 2):
             ycopy(n, i).wait_recv()
-            part[n * 4 + 3, s] += yrecv[n, s]
+            part(n * 4 + 3, s)[...] += yrecv[n, s]
         if i < 3:
 
             @pl.when(~inner)
@@ -334,12 +369,15 @@
             zarrive(n, s, s - z + 4 * zdir(i))
             zcopy(n, i).start()
 
-    def fcopy(j, n):
+    def fcopy(j, n, r=0):
         q, dev = ((t, yq), (t, cq), (yq, cq))[j]
         sl = pl.ds(pl.multiple_of(q * 512 + n * NB, NB), NB)
-        return _rcopy(yb.at[:, sl], yb.at[:, sl], fsem.at[0, n, j], fsem.at[1, n, j], {"tp": dev})
-
-    def finish(n):
+        rs = pl.ds(r * HR, HR) if n else pl.ds(0, tl)
+        return _rcopy(yb.at[rs, sl], yb.at[rs, sl], fsem.at[0, n + r, j], fsem.at[1, n + r, j], {"tp": dev})
+
+    pieces = ((0, 0),) + tuple((1, r) for r in range(tl // HR))
+
+    def zfinish(n):
         @pl.when(z > 0)
         def _():
             zarrive(n, z, 0)
@@ -348,11 +386,15 @@
         def _():
             zarrive(n, z, 4)
 
-        yb[:, pl.ds(pl.multiple_of(t * 512 + n * NB, NB), NB)] = part[n * 4 + 3, z].astype(BF)
-
-    def spread(n):
-        fcopy(0, n).start()
-        fcopy(1, n).start()
+    def spread(n, r=0):
+        rs = pl.ds(r * HR, HR) if n else pl.ds(0, tl)
+        v = part(n * 4 + 3, z)[rs, :]
+        if n:
+            hcopy(r).wait_recv()
+            v += yrecv[1, z, rs, :]
+        yb[rs, pl.ds(pl.multiple_of(t * 512 + n * NB, NB), NB)] = v.astype(BF)
+        fcopy(0, n, r).start()
+        fcopy(1, n, r).start()
 
     compute(0, 0)
     compute(0, 1)
@@ -361,12 +403,13 @@
     zacc(0, 2)
     zacc(0, 0)
     compute(1, 0)
-    zacc(0, 1)
     compute(1, 1)
     zfirst().wait_recv()
-    part[1, z] += zfrecv[...]
+    part(1, z)[...] += zfrecv[...]
     ycopy(0, 3).start()
-    ycopy(1, 3).start()
+    for r in range(tl // HR):
+        hcopy(r).start()
+    zacc(0, 1)
     relay(0, 0)
     compute(1, 2)
     compute(1, 3)
@@ -379,38 +422,52 @@
     relay(1, 1)
     zacc(0, 3)
     relay(1, 2)
-    finish(0)
+    zfinish(0)
     spread(0)
-    zacc(1, 3)
-    finish(1)
-    spread(1)
-    for n in range(2):
-        fcopy(0, n).wait_recv()
-        fcopy(2, n).start()
+    zfinish(1)
+    for n, r in pieces[1:]:
+        spread(n, r)
+    for n, r in pieces:
+        fcopy(0, n, r).wait_recv()
+        fcopy(2, n, r).start()
 
     @pl.loop(0, nu)
     def _(c):
         for kind in range(4):
             for i in range(3):
-                xcopy(kind, c, i).wait_send()
-
-    for i in range(3):
-        rcopy(i).wait_send()
+                if (kind, i) != (0, 0):
+                    xcopy(kind, c, i).wait_send()
+
+        @pl.when(inner)
+        def _():
+            xcopy(0, c, 0).wait_send()
+            xpass(c).wait_send()
+
+    rcopy(1).wait_send()
+    rcopy(2).wait_send()
+
+    @pl.when(inner)
+    def _():
+        rcopy(0).wait_send()
+        rpass().wait_send()
+
     for n in range(2):
         for i in range(4):
             for j in range(2):
                 dcopy(n, j, i).wait_send()
-            if (n, i) != (0, 2):
+            if (n, i) not in ((0, 2), (1, 3)):
                 ycopy(n, i).wait_send()
             if i < 3:
                 zcopy(n, i).wait_send()
     zfirst().wait_send()
-    for n in range(2):
-        fcopy(1, n).wait_recv()
-        fcopy(2, n).wait_recv()
-    for n in range(2):
+    for r in range(tl // HR):
+        hcopy(r).wait_send()
+    for n, r in pieces:
+        fcopy(1, n, r).wait_recv()
+        fcopy(2, n, r).wait_recv()
+    for n, r in pieces:
         for j in range(3):
-            fcopy(j, n).wait_send()
+            fcopy(j, n, r).wait_send()
     out = pltpu.make_async_copy(yb, y_ref, lsem.at[0])
     out.start()
     out.wait()
@@ -440,19 +497,19 @@
                 pltpu.VMEM((nep, el * cap, tl), BF),
                 pltpu.VMEM((nep, 3, tl, el * cap), BF),
                 pltpu.VMEM((el, nep * cap, CU), BF),
-                pltpu.VMEM((el, 2 * fl, nep * cap), F32),
+                pltpu.VMEM((el * 2 * fl, NB), F32),
                 pltpu.VMEM((el, nep * cap, fl), BF),
                 pltpu.VMEM((SL, EB, 2 * fl, CU), BF),
                 pltpu.VMEM((2, el, fl, NB), BF),
-                pltpu.VMEM((8, nep, tl, NB), F32),
                 pltpu.VMEM((2, 2, nep, tl, NB), F32),
                 pltpu.VMEM((2, nep, tl, NB), F32),
                 pltpu.VMEM((2, 5, tl, NB), F32),
                 pltpu.VMEM((tl, NB), F32),
                 pltpu.VMEM((tl, d), BF),
                 dma((1,)),
-                dma((2, 3)),
+                dma((2, 4)),
                 dma((8, nu, 3)),
+                dma((nu,)),
                 dma((2, SL)),
                 dma((2,)),
                 dma((2, 2, 2, 4)),
@@ -460,7 +517,8 @@
                 dma((2, 3)),
                 dma((2, 5)),
                 dma((2,)),
-                dma((2, 2, 3)),
+                dma((2, 5, 3)),
+                dma((2, tl // HR)),
             ],
             compiler_params=pltpu.CompilerParams(
                 collective_id=0, has_side_effects=True, vmem_limit_bytes=VMEM_LIMIT

time: 111 us -> 107 us (0.964)
  Pallas kernels: 109 us -> 104 us
    pallas_call x1, Pallas kernels: 109 us -> 104 us  [body(): pl.pallas_call(functools.partial(_moe_kernel, k, cap), out_shape=jax.Shap...]
where the time goes in v4:
time: 107 us; the launch traced here: 106 us
  Pallas kernels  104 us (97%)
  local copies, waits for them, and re-layouts  2.3 us (2%)
    pallas_call x1, Pallas kernels, body(): pl.pallas_call(functools.partial(_moe_kernel, k, cap), out_shape=jax.Shap...  104 us
    unnamed x1, local copies, waits for them, and re-layouts  2.3 us

profile of v4, /device:TPU:0, one launch (start us, length us, event | category | flops | bytes accessed | tf_op | source)
XLA Modules:
  0.0 106.4 jit_solution(2056453556067039903)
XLA Ops:
  0.0 104.1 %shard_map.64 = bf16[256,2048]{1,0:T(8,128)(2,1)} custom-call(bf16[256,2048]{1,0:T(8,128)(2,1)} %x_ref.1, s32[6,256]{1,0:T(8,128)} %bitcast.6, f32[6,256]{1,0:T(8,128)} %bitcast.7, bf16[16,352,2048]{2,1,0:T(8,128)(2,1)} %bitcast.4, bf16[16,352,2048]{2,1,0:T(8,128)(2,1)} %bitcast.5, bf16[16,352,2048]{2,1,0:T(8,128)(2,1)} %w2_ref.1), custom_call_target="tpu_custom_call" | custom-call | tf_op jit(solution)/shard_map/pallas_call | solution.py:489
  104.1 2.3 %copy.8 = bf16[256,2048]{1,0:T(8,128)(2,1)} copy(bf16[256,2048]{1,0:T(8,128)(2,1)} %shard_map.64) | data formatting | bytes 2097152

commit v5 on v4

--- a/solution.py
+++ b/solution.py
@@ -61,20 +61,9 @@
 
 NB = 256
 UN = 256
-CU = 512
-FWD = {
-    (0, 1): ((0, 4), (1, 1), (2, 3)),
-    (0, 3): ((0, 5), (1, 2), (2, 4)),
-    (1, 1): ((0, 6), (1, 3), (2, 5)),
-    (1, 3): ((0, 7), (1, 4), (2, 6)),
-    (2, 0): ((1, 5), (2, 7)),
-    (2, 2): ((1, 6),),
-    (3, 0): ((1, 7),),
-}
-UNITS = ((0, 1), (1, 2), (3, 2), (5, 2), (7, 1))
 HR = 64
-EB = 4
-SL = 4
+EB = 8
+SL = 3
 NT = (((1,), (1,)), ((), ()))
 
 
@@ -99,17 +88,14 @@
     def part(b, s):
         return hp.at[pl.ds(pl.multiple_of((b * ns + s) * tl, tl), tl), :]
 
-    wsteps = [(j, g) for j in range(len(UNITS)) for g in range(ng)]
-
     def wcopies(step):
-        j, g = wsteps[step]
-        u0, n = UNITS[j]
-        sl = step % SL
-        cs, ws = pl.ds(u0 * UN, n * UN), pl.ds(0, n * UN)
+        c, g = step // ng, lax.rem(step, ng)
+        sl = lax.rem(step, SL)
+        cs = pl.ds(pl.multiple_of(c * UN, UN), UN)
         es = pl.ds(g * EB, EB)
         return (
-            pltpu.make_async_copy(w1_ref.at[es, :, cs], wb.at[sl, :, pl.ds(0, fl), ws], wsem.at[0, sl]),
-            pltpu.make_async_copy(w3_ref.at[es, :, cs], wb.at[sl, :, pl.ds(fl, fl), ws], wsem.at[1, sl]),
+            pltpu.make_async_copy(w1_ref.at[es, :, cs], wb.at[sl, :, pl.ds(0, fl)], wsem.at[0, sl]),
+            pltpu.make_async_copy(w3_ref.at[es, :, cs], wb.at[sl, :, pl.ds(fl, fl)], wsem.at[1, sl]),
         )
 
     def wstart(step):
@@ -247,32 +233,46 @@
     yforward(0)
     znear(2)
 
-    for j, (u0, un) in enumerate(UNITS):
-        for u in range(u0, u0 + un):
-            xarrive(u)
-        cs = pl.ds(u0 * UN, un * UN)
+    def when(cond, f):
+        if isinstance(cond, bool):
+            if cond:
+                f()
+        else:
+            pl.when(cond)(f)
+
+    def multiply(u, first, last):
+        xarrive(u)
+        cs = pl.ds(pl.multiple_of(u * UN, UN), UN)
         for s in range(ns):
             v = jnp.dot(pm[s], xb[s, :, cs], preferred_element_type=F32).astype(BF)
-            xe[:, s * cap : (s + 1) * cap, 0 : un * UN] = v.reshape(el, cap, un * UN)
+            xe[:, s * cap : (s + 1) * cap, :] = v.reshape(el, cap, UN)
         for g in range(ng):
-            step = j * ng + g
-            for f, u in FWD.get((j, g), ()):
-                (zfar, yforward, znear)[f](u)
+            step = u * ng + g
+            if g == ng - 1 and not last:
+                when(u + 4 < nu, lambda: zfar(u + 4))
+                yforward(u + 1)
+                when(u + 3 < nu, lambda: znear(u + 3))
             for w in wcopies(step):
                 w.wait()
-            if step + SL - 1 < len(wsteps):
-                wstart(step + SL - 1)
+            when(step + SL - 1 < nu * ng, lambda: wstart(step + SL - 1))
+            sl = lax.rem(step, SL)
             for i in range(EB):
                 e = g * EB + i
-                v = lax.dot_general(
-                    wb[step % SL, i, :, 0 : un * UN], xe[e, :, 0 : un * UN], NT, preferred_element_type=F32
-                )
-                if j > 0:
+                v = lax.dot_general(wb[sl, i], xe[e], NT, preferred_element_type=F32)
+                if not first:
                     v += hacc(e)[...]
-                if j < len(UNITS) - 1:
+                if not last:
                     hacc(e)[...] = v
                 else:
                     hb[e] = (jax.nn.silu(v[:fl]) * v[fl:]).T.astype(BF)
+
+    multiply(0, True, False)
+
+    @pl.loop(1, nu - 1)
+    def _(u):
+        multiply(u, False, False)
+
+    multiply(nu - 1, False, True)
 
     def sof(i):
         far = (3 - i) * (1 - side) + i * side
@@ -400,7 +400,6 @@
     compute(0, 1)
     compute(0, 2)
     compute(0, 3)
-    zacc(0, 2)
     zacc(0, 0)
     compute(1, 0)
     compute(1, 1)
@@ -413,11 +412,12 @@
     relay(0, 0)
     compute(1, 2)
     compute(1, 3)
+    zacc(1, 0)
     relay(0, 1)
-    zacc(1, 0)
     zacc(1, 1)
+    relay(1, 0)
+    zacc(0, 2)
     relay(0, 2)
-    relay(1, 0)
     zacc(1, 2)
     relay(1, 1)
     zacc(0, 3)
@@ -496,10 +496,10 @@
                 pltpu.VMEM((nep, 16, tl), F32),
                 pltpu.VMEM((nep, el * cap, tl), BF),
                 pltpu.VMEM((nep, 3, tl, el * cap), BF),
-                pltpu.VMEM((el, nep * cap, CU), BF),
+                pltpu.VMEM((el, nep * cap, UN), BF),
                 pltpu.VMEM((el * 2 * fl, NB), F32),
                 pltpu.VMEM((el, nep * cap, fl), BF),
-                pltpu.VMEM((SL, EB, 2 * fl, CU), BF),
+                pltpu.VMEM((SL, EB, 2 * fl, UN), BF),
                 pltpu.VMEM((2, el, fl, NB), BF),
                 pltpu.VMEM((2, 2, nep, tl, NB), F32),
                 pltpu.VMEM((2, nep, tl, NB), F32),

time: 107 us -> 103 us (0.963)
  Pallas kernels: 104 us -> 101 us
    pallas_call x1, Pallas kernels: 104 us -> 101 us  [body(): pl.pallas_call(functools.partial(_moe_kernel, k, cap), out_shape=jax.Shap...]
where the time goes in v5:
time: 103 us
  Pallas kernels  101 us (98%)
  local copies, waits for them, and re-layouts  2.3 us (2%)
    pallas_call x1, Pallas kernels, body(): pl.pallas_call(functools.partial(_moe_kernel, k, cap), out_shape=jax.Shap...  101 us
    unnamed x1, local copies, waits for them, and re-layouts  2.3 us

profile of v5, /device:TPU:0, one launch (start us, length us, event | category | flops | bytes accessed | tf_op | source)
XLA Modules:
  0.0 103.0 jit_solution(5175168775040784061)
XLA Ops:
  0.0 100.6 %shard_map.64 = bf16[256,2048]{1,0:T(8,128)(2,1)} custom-call(bf16[256,2048]{1,0:T(8,128)(2,1)} %x_ref.1, s32[6,256]{1,0:T(8,128)} %bitcast.6, f32[6,256]{1,0:T(8,128)} %bitcast.7, bf16[16,352,2048]{2,1,0:T(8,128)(2,1)} %bitcast.4, bf16[16,352,2048]{2,1,0:T(8,128)(2,1)} %bitcast.5, bf16[16,352,2048]{2,1,0:T(8,128)(2,1)} %w2_ref.1), custom_call_target="tpu_custom_call" | custom-call | tf_op jit(solution)/shard_map/pallas_call | solution.py:489
  100.7 2.3 %copy.8 = bf16[256,2048]{1,0:T(8,128)(2,1)} copy(bf16[256,2048]{1,0:T(8,128)(2,1)} %shard_map.64) | data formatting | bytes 2097152

commit v6 on v5

--- a/solution.py
+++ b/solution.py
@@ -249,8 +249,8 @@
         for g in range(ng):
             step = u * ng + g
             if g == ng - 1 and not last:
+                yforward(u + 1)
                 when(u + 4 < nu, lambda: zfar(u + 4))
-                yforward(u + 1)
                 when(u + 3 < nu, lambda: znear(u + 3))
             for w in wcopies(step):
                 w.wait()
@@ -297,9 +297,9 @@
         w2copy(b).wait()
         sl = b % 2
 
-        @pl.loop(0, el, step=8)
+        @pl.loop(0, el, step=16)
         def _(e0):
-            for i in range(8):
+            for i in range(16):
                 e = e0 + i
                 v = jnp.dot(hb[e], w2b[sl, e], preferred_element_type=F32).astype(BF)
                 pm[:, pl.ds(pl.multiple_of(e * cap, cap), cap), :] = v.reshape(ns, cap, NB)

time: 103 us -> 102 us (level)
  Pallas kernels: 101 us -> 99.7 us
where the time goes in v6:
time: 102 us
  Pallas kernels  99.7 us (98%)
  local copies, waits for them, and re-layouts  2.3 us (2%)
    pallas_call x1, Pallas kernels, body(): pl.pallas_call(functools.partial(_moe_kernel, k, cap), out_shape=jax.Shap...  99.7 us
    unnamed x1, local copies, waits for them, and re-layouts  2.3 us

profile of v6, /device:TPU:0, one launch (start us, length us, event | category | flops | bytes accessed | tf_op | source)
XLA Modules:
  0.0 102.0 jit_solution(15529436619928666951)
XLA Ops:
  0.0 99.7 %shard_map.64 = bf16[256,2048]{1,0:T(8,128)(2,1)} custom-call(bf16[256,2048]{1,0:T(8,128)(2,1)} %x_ref.1, s32[6,256]{1,0:T(8,128)} %bitcast.6, f32[6,256]{1,0:T(8,128)} %bitcast.7, bf16[16,352,2048]{2,1,0:T(8,128)(2,1)} %bitcast.4, bf16[16,352,2048]{2,1,0:T(8,128)(2,1)} %bitcast.5, bf16[16,352,2048]{2,1,0:T(8,128)(2,1)} %w2_ref.1), custom_call_target="tpu_custom_call" | custom-call | tf_op jit(solution)/shard_map/pallas_call | solution.py:489
  99.7 2.3 %copy.8 = bf16[256,2048]{1,0:T(8,128)(2,1)} copy(bf16[256,2048]{1,0:T(8,128)(2,1)} %shard_map.64) | data formatting | bytes 2097152
